TPU v7x, 32 devices: a whole 2x2x4 slice. The times are simulated.
32 devices in a mesh: row: 8 (over z, x), col: 2 (over y), rep: 2 (over core).
Axes of the slice: x: 2, y: 2, z: 4, core: 2. Of those that a mesh axis runs over, the one named last changes fastest.
Arguments:
- matrix: float32 [16384, 16384], P('row', 'col'), may hold values from -0.125 to 0.125
- vectors: float32 [64, 16384], P('rep', 'row'), may hold values from -0.3 to 0.3
Outputs:
- result: float32 [64, 16384], P('rep', 'row')
All inputs are finite; a program needn't handle non-finite values.
Results may differ from a plain program's by a relative error of at most 0.00011.
Values sent between devices are 32-bit elements; how exact they have to be, the bound alone decides.
A program may use at most 128 MiB of HBM per device.

v0:
```python
import functools

import jax
import jax.numpy as jnp
from jax import lax
from jax.experimental import pallas as pl
from jax.experimental.pallas import tpu as pltpu
from jax.sharding import PartitionSpec as P

TERMS = 6
STEPS = 1
MESH = pl.DeviceIdType.MESH
TILE = 256
SLOTS = 4
LAG = 5
SPLIT = 2


def kernel(
    rows, cols, m_ref, v_ref, out_ref,
    high, low, stage, xbuf, acc, drecv, ybuf, run, fin, frecv,
    stage_sem, init_send, init_recv, x_recv, up_send, down_send, pair_send,
    d_send, d_recv, y_send, y_recv, f_send, f_recv,
):
    fanout = rows // cols
    size = m_ref.shape[0]
    share = v_ref.shape[0]
    half = size // 2
    chunks = half // TILE
    tiles = size // TILE
    lines = rows // 2
    depth = fanout // 2
    total = fanout * chunks

    r, c, p = lax.axis_index("row"), lax.axis_index("col"), lax.axis_index("rep")
    z, x = r // 2, r % 2
    first_line = c * depth
    owner = r // fanout
    own = owner == c
    mine = r % fanout

    barrier = pltpu.get_barrier_semaphore()

    def greet(**where):
        pl.semaphore_signal(barrier, inc=1, device_id=where, device_id_type=MESH)

    greet(rep=1 - p)
    greet(row=z * 2 + 1 - x)
    for offset in range(1, cols):
        greet(col=(c + offset) % cols)

    @pl.when(z > 0)
    def _():
        greet(row=r - 2)

    @pl.when(z < lines - 1)
    def _():
        greet(row=r + 2)

    def chunk_of(step):
        count = total // 2
        lag = min(LAG, count)
        mixed = step - lag
        alternate = jnp.where(mixed % 2 == 0, count + mixed // 2, lag + mixed // 2)
        place = jnp.where(step < lag, step, jnp.where(step < 2 * count - lag, alternate, step))
        other, place = place // count, place % count
        near = place // chunks
        line = jnp.where(z > first_line, depth - 1 - near, near)
        lane = jnp.where(other == 0, x, 1 - x)
        return line, lane, line * 2 + lane, place % chunks

    def load(step):
        _, _, j, k = chunk_of(step)
        start = pl.multiple_of(j * size + p * half + k * TILE, TILE)
        return pltpu.make_async_copy(
            m_ref.at[:, pl.ds(start, TILE)], stage.at[step % SLOTS], stage_sem.at[step % SLOTS]
        )

    for step in range(min(SLOTS, total)):
        load(step).start()

    pl.semaphore_wait(barrier, 1 + cols + (z > 0).astype(jnp.int32) + (z < lines - 1).astype(jnp.int32))

    def remote(source, target, send, recv, **where):
        return pltpu.make_async_remote_copy(
            src_ref=source, dst_ref=target, send_sem=send, recv_sem=recv,
            device_id=where, device_id_type=MESH,
        )

    part = share * 2 // SPLIT

    def hops(s, line, lane, j, k, h):
        ref, recv = xbuf.at[s, j, k, pl.ds(h * part, part), :], x_recv.at[s % 2, j, k, h]
        here = lane == x
        return (
            (here & (z >= line) & (z < lines - 1), remote(ref, ref, up_send.at[j, k, h], recv, row=r + 2)),
            (here & (z <= line) & (z > 0), remote(ref, ref, down_send.at[j, k, h], recv, row=r - 2)),
            (here, remote(ref, ref, pair_send.at[j, k, h], recv, row=z * 2 + 1 - x)),
        )

    def pass_on(s, line, lane, j, k, h, again):
        for needed, copy in hops(s, line, lane, j, k, h):
            @pl.when(needed)
            def _(copy=copy):
                if again:
                    copy.wait_send()
                copy.start()

    def pass_own(s, k, h, again):
        pass_on(s, z, x, mine, k, h, again)

    @pl.when(own)
    def _():
        def given(k):
            start = pl.multiple_of((1 - p) * half + k * TILE, TILE)
            return remote(
                v_ref.at[:, pl.ds(start, TILE)],
                xbuf.at[0, mine, k, pl.ds(pl.multiple_of(p * share, share), share), :],
                init_send.at[k], init_recv.at[k], rep=1 - p,
            )

        for k in range(chunks):
            given(k).start()
        for k in range(chunks):
            start = pl.multiple_of(p * half + k * TILE, TILE)
            xbuf[0, mine, k, pl.ds(pl.multiple_of(p * share, share), share), :] = v_ref[:, pl.ds(start, TILE)]
        for k in range(chunks):
            given(k).wait()
            run[k] = xbuf[0, mine, k]
            for h in range(SPLIT):
                pass_own(0, k, h, False)

    @pl.when(jnp.logical_not(own))
    def _():
        run[...] = jnp.zeros_like(run)

    def prepare(step, index):
        load(step).wait()
        for n in range(tiles):
            block = stage[step % SLOTS, n * TILE:(n + 1) * TILE, :]
            top = block.astype(jnp.bfloat16)
            rest = (block - top.astype(jnp.float32)).astype(jnp.bfloat16)
            high[index, n] = top.T
            low[index, n] = rest.T

        @pl.when(step + SLOTS < total)
        def _():
            load(step + SLOTS).start()

    def multiply(s, first):
        acc[...] = jnp.zeros_like(acc)

        def body(step, carry):
            line, lane, j, k = chunk_of(step)
            index = j * chunks + k
            if first:
                prepare(step, index)

            @pl.when(r != c * fanout + j)
            def _():
                for h in range(SPLIT):
                    ref = xbuf.at[s, j, k, pl.ds(h * part, part), :]
                    remote(ref, ref, up_send.at[j, k, h], x_recv.at[s % 2, j, k, h], rep=1 - p).wait_recv()
                    pass_on(s, first_line + line, lane, j, k, h, not first)

            value = xbuf[s, j, k]
            top = value.astype(jnp.bfloat16)
            rest = (value - top.astype(jnp.float32)).astype(jnp.bfloat16)
            both = jnp.concatenate([top, rest], axis=0)
            count = value.shape[0]
            for n in range(tiles):
                large = jnp.dot(both, high[index, n], preferred_element_type=jnp.float32)
                small = jnp.dot(top, low[index, n], preferred_element_type=jnp.float32)
                acc[n] += large[:count] + (large[count:] + small)
            return carry

        lax.fori_loop(0, total, body, 0)

    def swap(s, k):
        return remote(
            acc.at[(1 - p) * chunks + k], drecv.at[s, k], d_send.at[k], d_recv.at[s % 2, k], rep=1 - p
        )

    def to_column(s, k, h, target):
        ref = ybuf.at[s, c, k, pl.ds(h * part, part), :]
        return remote(ref, ref, y_send.at[target, k, h], y_recv.at[s % 2, c, k, h], col=target)

    def from_column(s, k, h, source):
        ref = ybuf.at[s, source, k, pl.ds(h * part, part), :]
        return remote(ref, ref, y_send.at[source, k, h], y_recv.at[s % 2, source, k, h], col=source)

    def column_sum(s, k, h):
        for offset in range(1, cols):
            from_column(s, k, h, (c + offset) % cols).wait_recv()
        value = ybuf[s, 0, k, h * part:(h + 1) * part, :]
        for source in range(1, cols):
            value = value + ybuf[s, source, k, h * part:(h + 1) * part, :]
        return value

    def scaled(s, k):
        swap(s, k).wait_recv()
        degree = jnp.asarray((s + 1) * STEPS, jnp.int32).astype(jnp.float32)
        return (acc[p * chunks + k] + drecv[s, k]) / degree

    def reduce(s, first):
        for k in range(chunks):
            swap(s, k).start()

        @pl.when(own)
        def _():
            for k in range(chunks):
                ybuf[s, c, k] = scaled(s, k)
                for h in range(SPLIT):
                    piece = slice(h * part, (h + 1) * part)
                    value = column_sum(s, k, h)
                    xbuf[s + 1, mine, k, piece, :] = value
                    run[k, piece, :] = run[k, piece, :] + value
                    pass_own(s + 1, k, h, True)

        @pl.when(jnp.logical_not(own))
        def _():
            for k in range(chunks):
                ybuf[s, c, k] = scaled(s, k)
                for h in range(SPLIT):
                    if not first:
                        to_column(s, k, h, owner).wait_send()
                    to_column(s, k, h, owner).start()

        for k in range(chunks):
            swap(s, k).wait_send()

    multiply(0, True)
    reduce(0, True)

    def middle(s, carry):
        multiply(s, False)
        reduce(s, False)
        return carry

    lax.fori_loop(1, TERMS - 1, middle, 0)

    last = TERMS - 1
    multiply(last, False)
    for k in range(chunks):
        swap(last, k).start()
    for k in range(chunks):
        ybuf[last, c, k] = scaled(last, k) + run[k]

        @pl.when(jnp.logical_not(own))
        def _(k=k):
            for h in range(SPLIT):
                to_column(last, k, h, owner).wait_send()

        for offset in range(1, cols):
            for h in range(SPLIT):
                to_column(last, k, h, (c + offset) % cols).start()

    def give(k):
        theirs = pl.ds(pl.multiple_of((1 - p) * share, share), share)
        return remote(fin.at[k, theirs, :], frecv.at[k], f_send.at[k], f_recv.at[k], rep=1 - p)

    for k in range(chunks):
        for h in range(SPLIT):
            fin[k, h * part:(h + 1) * part, :] = column_sum(last, k, h)
        give(k).start()
        start = pl.multiple_of(p * half + k * TILE, TILE)
        out_ref[:, pl.ds(start, TILE)] = fin[k, pl.ds(pl.multiple_of(p * share, share), share), :]
    for k in range(chunks):
        give(k).wait()
        start = pl.multiple_of((1 - p) * half + k * TILE, TILE)
        out_ref[:, pl.ds(start, TILE)] = frecv[k]

    for k in range(chunks):
        swap(last, k).wait_send()
        for offset in range(1, cols):
            for h in range(SPLIT):
                to_column(last, k, h, (c + offset) % cols).wait_send()

    def drain(step, carry):
        line, lane, j, k = chunk_of(step)
        for h in range(SPLIT):
            for needed, copy in hops(last, first_line + line, lane, j, k, h):
                @pl.when(needed)
                def _(copy=copy):
                    copy.wait_send()
        return carry

    lax.fori_loop(0, total, drain, 0)


def solution(mesh):
    rows, cols, reps = (mesh.shape[axis] for axis in ("row", "col", "rep"))

    def local(matrix, vectors):
        size, width = matrix.shape
        share = vectors.shape[0]
        every = share * reps
        fanout = rows // cols
        chunks = size // 2 // TILE
        tiles = size // TILE
        piece = (every, TILE)
        dma = pltpu.SemaphoreType.DMA
        return pl.pallas_call(
            functools.partial(kernel, rows, cols),
            out_shape=jax.ShapeDtypeStruct(vectors.shape, jnp.float32),
            in_specs=[pl.BlockSpec(memory_space=pltpu.HBM), pl.BlockSpec(memory_space=pltpu.VMEM)],
            out_specs=pl.BlockSpec(memory_space=pltpu.VMEM),
            scratch_shapes=[
                pltpu.VMEM((fanout * chunks, tiles, TILE, TILE), jnp.bfloat16),
                pltpu.VMEM((fanout * chunks, tiles, TILE, TILE), jnp.bfloat16),
                pltpu.VMEM((SLOTS, size, TILE), jnp.float32),
                pltpu.VMEM((TERMS, fanout, chunks) + piece, jnp.float32),
                pltpu.VMEM((tiles,) + piece, jnp.float32),
                pltpu.VMEM((TERMS, chunks) + piece, jnp.float32),
                pltpu.VMEM((TERMS, cols, chunks) + piece, jnp.float32),
                pltpu.VMEM((chunks,) + piece, jnp.float32),
                pltpu.VMEM((chunks,) + piece, jnp.float32),
                pltpu.VMEM((chunks, share, TILE), jnp.float32),
                dma((SLOTS,)),
                dma((chunks,)),
                dma((chunks,)),
                dma((2, fanout, chunks, SPLIT)),
                dma((fanout, chunks, SPLIT)),
                dma((fanout, chunks, SPLIT)),
                dma((fanout, chunks, SPLIT)),
                dma((chunks,)),
                dma((2, chunks)),
                dma((cols, chunks, SPLIT)),
                dma((2, cols, chunks, SPLIT)),
                dma((chunks,)),
                dma((chunks,)),
            ],
            compiler_params=pltpu.CompilerParams(
                collective_id=0, has_side_effects=True, vmem_limit_bytes=63 * 1024 * 1024
            ),
        )(matrix, vectors)

    return jax.shard_map(
        local, mesh=mesh, in_specs=(P("row", "col"), P("rep", "row")), out_specs=P("rep", "row"), check_vma=False
    )
```

profile of v0, /device:TPU:0, one launch (start us, length us, event | category | flops | bytes accessed | tf_op | source)
XLA Modules:
  0.0 154.7 jit_solution(16738812355299390917)
XLA Ops:
  0.0 153.0 %shard_map.28 = f32[32,2048]{1,0:T(8,128)} custom-call(f32[2048,8192]{1,0:T(8,128)} %m_ref.1, f32[32,2048]{1,0:T(8,128)} %v_ref.1), custom_call_target="tpu_custom_call" | custom-call | tf_op jit(solution)/shard_map/pallas_call | solution.py:303
  153.0 1.7 %copy.4 = f32[32,2048]{1,0:T(8,128)} copy(f32[32,2048]{1,0:T(8,128)} %shard_map.28) | data formatting | bytes 524288
where the time goes:
time: 155 us
  Pallas kernels  153 us (99%)
  local copies, waits for them, and re-layouts  1.67 us (1%)
    pallas_call x1, Pallas kernels, local(): pl.pallas_call(functools.partial(kernel, rows, cols), out_shape=jax.Shape...  153 us

commit v1 on v0

v1 whole, which is shorter than its diff:
```python
import functools

import jax
import jax.numpy as jnp
from jax import lax
from jax.experimental import pallas as pl
from jax.experimental.pallas import tpu as pltpu
from jax.sharding import PartitionSpec as P

TERMS = 6
STEPS = 1
MESH = pl.DeviceIdType.MESH
TILE = 256
SLOTS = 4
LAG = 5
SUM_AT = 3


def kernel(rows, cols, groups, *refs):
    tiles = refs[0].shape[0] // TILE
    part = refs[1].shape[0]
    sums = [pltpu.ACC(n % 2)((part, TILE), jnp.float32) for n in range(tiles)]
    pl.run_scoped(lambda *sums: body(rows, cols, groups, sums, *refs), *sums)


def body(
    rows, cols, groups, sums, m_ref, v_ref, out_ref,
    high, low, stage, xbuf, sbuf, acc, drecv, ybuf, run, fin, frecv,
    stage_sem, init_send, init_recv, x_recv, line_send, pair_send,
    d_send, d_recv, y_send, y_recv, f_send, f_recv,
):
    fanout = rows // cols
    size = m_ref.shape[0]
    part = v_ref.shape[0]
    half = size // 2
    chunks = half // TILE
    tiles = size // TILE
    lines = rows // 2
    depth = fanout // 2
    total = fanout * chunks
    last = TERMS - 1

    r, c, p = lax.axis_index("row"), lax.axis_index("col"), lax.axis_index("rep")
    z, x = r // 2, r % 2
    first_line = c * depth
    owner = r // fanout
    own = owner == c
    helper = (owner + 1) % cols
    aid = (helper == c) & (depth > 1)
    mine = r % fanout

    barrier = pltpu.get_barrier_semaphore()

    def greet(**where):
        pl.semaphore_signal(barrier, inc=1, device_id=where, device_id_type=MESH)

    greet(rep=1 - p)
    greet(row=z * 2 + 1 - x)
    for other in range(1, lines * cols):
        greet(row=(z + other // cols) % lines * 2 + x, col=(c + other % cols) % cols)

    def chunk_of(step):
        count = total // 2
        lag = min(LAG, count)
        mixed = step - lag
        alternate = jnp.where(mixed % 2 == 0, count + mixed // 2, lag + mixed // 2)
        place = jnp.where(step < lag, step, jnp.where(step < 2 * count - lag, alternate, step))
        other, place = place // count, place % count
        near = jnp.where(own, place // chunks, place % depth)
        line = jnp.where(z > first_line, depth - 1 - near, near)
        lane = jnp.where(other == 0, x, 1 - x)
        return line, lane, line * 2 + lane, jnp.where(own, place % chunks, place // depth)

    def load(step):
        _, _, j, k = chunk_of(step)
        start = pl.multiple_of(j * size + p * half + k * TILE, TILE)
        return pltpu.make_async_copy(
            m_ref.at[:, pl.ds(start, TILE)], stage.at[step % SLOTS], stage_sem.at[step % SLOTS]
        )

    for step in range(min(SLOTS, total)):
        load(step).start()

    for total_ref in sums:
        pltpu.matmul_pop(total_ref)

    pl.semaphore_wait(barrier, lines * cols + 1)

    def remote(source, target, send, recv, **where):
        return pltpu.make_async_remote_copy(
            src_ref=source, dst_ref=target, send_sem=send, recv_sem=recv,
            device_id=where, device_id_type=MESH,
        )

    def relay(s, h, j, k):
        ref = xbuf.at[s, h, j, k]
        return remote(ref, ref, pair_send.at[h, j, k], x_recv.at[s % 2, h, j, k], row=z * 2 + 1 - x)

    def routes(s, h, k):
        first = owner * depth
        top = first + depth - 1
        source, target, recv = sbuf.at[s, h, k], xbuf.at[s, h, mine, k], x_recv.at[s % 2, h, mine, k]
        for t in range(lines):
            inside = (t >= first) & (t <= top)
            direct = inside | (jnp.where(t > top, top, first) == z)
            needed = (t != z) & ((own & direct) | (aid & jnp.logical_not(direct)))
            yield needed, remote(source, target, line_send.at[h, t, k], recv, row=t * 2 + x, col=owner)
        yield own, remote(source, target, pair_send.at[h, mine, k], recv, row=z * 2 + 1 - x)

    def spread(s, h, k, again):
        for needed, copy in routes(s, h, k):
            @pl.when(needed)
            def _(copy=copy):
                if again:
                    copy.wait_send()
                copy.start()

    @pl.when(own | aid)
    def _():
        def given(k):
            start = pl.multiple_of((1 - p) * half + k * TILE, TILE)
            return remote(
                v_ref.at[:, pl.ds(start, TILE)], sbuf.at[0, p, k], init_send.at[k], init_recv.at[k], rep=1 - p,
            )

        for k in range(chunks):
            given(k).start()
        for k in range(chunks):
            start = pl.multiple_of(p * half + k * TILE, TILE)
            sbuf[0, p, k] = v_ref[:, pl.ds(start, TILE)]
        for k in range(chunks):
            given(k).wait()
            spread(0, 0, k, False)
        for h in range(1, groups):
            for k in range(chunks):
                spread(0, h, k, False)

    @pl.when(own)
    def _():
        for h in range(groups):
            for k in range(chunks):
                run[h, k] = sbuf[0, h, k]
                xbuf[0, h, mine, k] = sbuf[0, h, k]

    @pl.when(jnp.logical_not(own))
    def _():
        run[...] = jnp.zeros_like(run)

    def prepare(step, index):
        load(step).wait()
        for n in range(tiles):
            block = stage[step % SLOTS, n * TILE:(n + 1) * TILE, :]
            top = block.astype(jnp.bfloat16)
            rest = (block - top.astype(jnp.float32)).astype(jnp.bfloat16)
            high[index, n] = top.T
            low[index, n] = rest.T

        @pl.when(step + SLOTS < total)
        def _():
            load(step + SLOTS).start()

    def gather(s, h, step, again):
        _, lane, j, k = chunk_of(step)

        @pl.when(r != c * fanout + j)
        def _():
            copy = relay(s, h, j, k)
            copy.wait_recv()

            @pl.when(lane == x)
            def _():
                if again:
                    copy.wait_send()
                copy.start()

    def multiply(s, h, step):
        _, _, j, k = chunk_of(step)
        index = j * chunks + k
        value = xbuf[s, h, j, k]
        top = value.astype(jnp.bfloat16)
        rest = (value - top.astype(jnp.float32)).astype(jnp.bfloat16)
        for n in range(tiles):
            pltpu.matmul_push_rhs(high[index, n], staging_register=0, mxu_index=n % 2)
            pltpu.matmul_acc_lhs(sums[n], top, load_staged_rhs=0)
            pltpu.matmul_acc_lhs(sums[n], rest)
            pltpu.matmul_push_rhs(low[index, n], staging_register=1, mxu_index=n % 2)
            pltpu.matmul_acc_lhs(sums[n], top, load_staged_rhs=1)

    def swap(s, h, k):
        return remote(
            acc.at[h, (1 - p) * chunks + k], drecv.at[s, h, k],
            d_send.at[h, k], d_recv.at[s % 2, h, k], rep=1 - p,
        )

    def close(s, h):
        for n in range(tiles):
            acc[h, n] = pltpu.matmul_pop(sums[n])
        for k in range(chunks):
            swap(s, h, k).start()

    def to_column(s, h, k, target):
        ref = ybuf.at[s, h, c, k]
        return remote(ref, ref, y_send.at[target, h, k], y_recv.at[s % 2, c, h, k], col=target)

    def from_column(s, h, k, source):
        ref = ybuf.at[s, h, source, k]
        return remote(ref, ref, y_send.at[source, h, k], y_recv.at[s % 2, source, h, k], col=source)

    def column_sum(s, h, k):
        for offset in range(1, cols):
            from_column(s, h, k, (c + offset) % cols).wait_recv()
        value = ybuf[s, h, 0, k]
        for source in range(1, cols):
            value = value + ybuf[s, h, source, k]
        return value

    def scaled(s, h, k):
        swap(s, h, k).wait_recv()
        degree = jnp.asarray((s + 1) * STEPS, jnp.int32).astype(jnp.float32)
        return (acc[h, p * chunks + k] + drecv[s, h, k]) / degree

    def to_makers(s, h, k, visit):
        for target, there in ((owner, True), (helper, depth > 1)):
            if there:
                @pl.when(c != target)
                def _(target=target):
                    visit(to_column(s, h, k, target))

    def add_up(s, h):
        for k in range(chunks):
            ybuf[s, h, c, k] = scaled(s, h, k)

            @pl.when(s > 0)
            def _(k=k):
                to_makers(s, h, k, lambda copy: copy.wait_send())

            to_makers(s, h, k, lambda copy: copy.start())

        @pl.when(aid)
        def _():
            for k in range(chunks):
                sbuf[s + 1, h, k] = column_sum(s, h, k)
                spread(s + 1, h, k, True)

    def send_out(s, h, k):
        @pl.when(own)
        def _():
            value = column_sum(s, h, k)
            sbuf[s + 1, h, k] = value
            spread(s + 1, h, k, True)
            xbuf[s + 1, h, mine, k] = value
            run[h, k] = run[h, k] + value

        swap(s, h, k).wait_send()

    def add_up_last(h):
        for k in range(chunks):
            ybuf[last, h, c, k] = scaled(last, h, k) + run[h, k]

            to_makers(last, h, k, lambda copy: copy.wait_send())
            for offset in range(1, cols):
                to_column(last, h, k, (c + offset) % cols).start()

    def give(k):
        return remote(fin.at[k], frecv.at[k], f_send.at[k], f_recv.at[k], rep=1 - p)

    def finish(h, k):
        value = column_sum(last, h, k)

        @pl.when(p == h)
        def _():
            start = pl.multiple_of(p * half + k * TILE, TILE)
            out_ref[:, pl.ds(start, TILE)] = value

        @pl.when(p != h)
        def _():
            fin[k] = value
            give(k).start()

        swap(last, h, k).wait_send()

    sum_at = SUM_AT * total // 16

    def opening(step, carry):
        _, _, j, k = chunk_of(step)
        prepare(step, j * chunks + k)
        gather(0, 0, step, False)
        multiply(0, 0, step)
        for h in range(1, groups):
            gather(0, h, step, False)
        return carry

    lax.fori_loop(0, total, opening, 0)
    close(0, 0)

    def loop(s, h, again, begin, each):
        def run_step(step, carry):
            if again:
                gather(s, h, step, True)
            multiply(s, h, step)

            @pl.when(step == sum_at)
            def _():
                begin()

            return carry

        lax.fori_loop(0, total, run_step, 0)
        close(s, h)
        for k in range(chunks):
            each(k)

    def behind(s, h):
        return functools.partial(add_up, s, h), functools.partial(send_out, s, h)

    for h in range(1, groups):
        loop(0, h, False, *behind(0, h - 1))

    def middle(s, carry):
        loop(s, 0, True, *behind(s - 1, groups - 1))
        for h in range(1, groups):
            loop(s, h, True, *behind(s, h - 1))
        return carry

    lax.fori_loop(1, last, middle, 0)
    loop(last, 0, True, *behind(last - 1, groups - 1))
    for h in range(1, groups):
        loop(last, h, True, functools.partial(add_up_last, h - 1), functools.partial(finish, h - 1))
    add_up_last(groups - 1)
    for k in range(chunks):
        finish(groups - 1, k)

    for k in range(chunks):
        give(k).wait()
        start = pl.multiple_of((1 - p) * half + k * TILE, TILE)
        out_ref[:, pl.ds(start, TILE)] = frecv[k]
        for h in range(groups):
            for offset in range(1, cols):
                to_column(last, h, k, (c + offset) % cols).wait_send()

    def drain(step, carry):
        _, lane, j, k = chunk_of(step)

        @pl.when(lane == x)
        def _():
            for h in range(groups):
                relay(last, h, j, k).wait_send()

        return carry

    lax.fori_loop(0, total, drain, 0)
    for h in range(groups):
        for k in range(chunks):
            for needed, copy in list(routes(last, h, k))[:-1]:
                @pl.when(needed)
                def _(copy=copy):
                    copy.wait_send()


def solution(mesh):
    rows, cols, groups = (mesh.shape[axis] for axis in ("row", "col", "rep"))

    def local(matrix, vectors):
        size, width = matrix.shape
        part = vectors.shape[0]
        fanout = rows // cols
        chunks = size // 2 // TILE
        tiles = size // TILE
        piece = (part, TILE)
        dma = pltpu.SemaphoreType.DMA
        return pl.pallas_call(
            functools.partial(kernel, rows, cols, groups),
            out_shape=jax.ShapeDtypeStruct(vectors.shape, jnp.float32),
            in_specs=[pl.BlockSpec(memory_space=pltpu.HBM), pl.BlockSpec(memory_space=pltpu.VMEM)],
            out_specs=pl.BlockSpec(memory_space=pltpu.VMEM),
            scratch_shapes=[
                pltpu.VMEM((fanout * chunks, tiles, TILE, TILE), jnp.bfloat16),
                pltpu.VMEM((fanout * chunks, tiles, TILE, TILE), jnp.bfloat16),
                pltpu.VMEM((SLOTS, size, TILE), jnp.float32),
                pltpu.VMEM((TERMS, groups, fanout, chunks) + piece, jnp.float32),
                pltpu.VMEM((TERMS, groups, chunks) + piece, jnp.float32),
                pltpu.VMEM((groups, tiles) + piece, jnp.float32),
                pltpu.VMEM((TERMS, groups, chunks) + piece, jnp.float32),
                pltpu.VMEM((TERMS, groups, cols, chunks) + piece, jnp.float32),
                pltpu.VMEM((groups, chunks) + piece, jnp.float32),
                pltpu.VMEM((chunks,) + piece, jnp.float32),
                pltpu.VMEM((chunks,) + piece, jnp.float32),
                dma((SLOTS,)),
                dma((chunks,)),
                dma((chunks,)),
                dma((2, groups, fanout, chunks)),
                dma((groups, rows // 2, chunks)),
                dma((groups, fanout, chunks)),
                dma((groups, chunks)),
                dma((2, groups, chunks)),
                dma((cols, groups, chunks)),
                dma((2, cols, groups, chunks)),
                dma((chunks,)),
                dma((chunks,)),
            ],
            compiler_params=pltpu.CompilerParams(
                collective_id=0, has_side_effects=True, vmem_limit_bytes=63 * 1024 * 1024
            ),
        )(matrix, vectors)

    return jax.shard_map(
        local, mesh=mesh, in_specs=(P("row", "col"), P("rep", "row")), out_specs=P("rep", "row"), check_vma=False
    )
```

time: 155 us -> 140 us (0.903)
  Pallas kernels: 153 us -> 138 us
    pallas_call x1, Pallas kernels: 153 us -> 138 us  [local(): pl.pallas_call(functools.partial(kernel, rows, cols, groups), out_shape=j...]
where the time goes in v1:
time: 140 us
  Pallas kernels  138 us (99%)
  local copies, waits for them, and re-layouts  1.67 us (1%)
    pallas_call x1, Pallas kernels, local(): pl.pallas_call(functools.partial(kernel, rows, cols, groups), out_shape=j...  138 us

profile of v1, /device:TPU:0, one launch (start us, length us, event | category | flops | bytes accessed | tf_op | source)
XLA Modules:
  0.0 140.1 jit_solution(7760399773720729081)
XLA Ops:
  0.0 138.4 %shard_map.28 = f32[32,2048]{1,0:T(8,128)} custom-call(f32[2048,8192]{1,0:T(8,128)} %refs_0_.1, f32[32,2048]{1,0:T(8,128)} %refs_1_.1), custom_call_target="tpu_custom_call" | custom-call | tf_op jit(solution)/shard_map/pallas_call | solution.py:371
  138.4 1.7 %copy.4 = f32[32,2048]{1,0:T(8,128)} copy(f32[32,2048]{1,0:T(8,128)} %shard_map.28) | data formatting | bytes 524288

commit v2 on v1

--- a/solution.py
+++ b/solution.py
@@ -14,6 +14,8 @@
 SLOTS = 4
 LAG = 5
 SUM_AT = 3
+HELP_AT = 6
+AHEAD = 1
 
 
 def kernel(rows, cols, groups, *refs):
@@ -65,17 +67,21 @@
         mixed = step - lag
         alternate = jnp.where(mixed % 2 == 0, count + mixed // 2, lag + mixed // 2)
         place = jnp.where(step < lag, step, jnp.where(step < 2 * count - lag, alternate, step))
-        other, place = place // count, place % count
+        return block_of(place // count, place % count)
+
+    def block_of(other, place):
         near = jnp.where(own, place // chunks, place % depth)
         line = jnp.where(z > first_line, depth - 1 - near, near)
         lane = jnp.where(other == 0, x, 1 - x)
         return line, lane, line * 2 + lane, jnp.where(own, place % chunks, place // depth)
 
-    def load(step):
-        _, _, j, k = chunk_of(step)
+    middle_step = total // 2
+
+    def load(turn):
+        _, _, j, k = chunk_of((turn + middle_step) % total)
         start = pl.multiple_of(j * size + p * half + k * TILE, TILE)
         return pltpu.make_async_copy(
-            m_ref.at[:, pl.ds(start, TILE)], stage.at[step % SLOTS], stage_sem.at[step % SLOTS]
+            m_ref.at[:, pl.ds(start, TILE)], stage.at[turn % SLOTS], stage_sem.at[turn % SLOTS]
         )
 
     for step in range(min(SLOTS, total)):
@@ -128,9 +134,18 @@
         for k in range(chunks):
             start = pl.multiple_of(p * half + k * TILE, TILE)
             sbuf[0, p, k] = v_ref[:, pl.ds(start, TILE)]
+        @pl.when(p == 0)
+        def _():
+            for k in range(chunks):
+                spread(0, 0, k, False)
+
         for k in range(chunks):
             given(k).wait()
-            spread(0, 0, k, False)
+
+            @pl.when(p != 0)
+            def _(k=k):
+                spread(0, 0, k, False)
+
         for h in range(1, groups):
             for k in range(chunks):
                 spread(0, h, k, False)
@@ -146,45 +161,67 @@
     def _():
         run[...] = jnp.zeros_like(run)
 
-    def prepare(step, index):
-        load(step).wait()
+    def feed(n, top, rest, large, small):
+        pltpu.matmul_push_rhs(large, staging_register=0, mxu_index=n % 2)
+        pltpu.matmul_acc_lhs(sums[n], top, load_staged_rhs=0)
+        pltpu.matmul_acc_lhs(sums[n], rest)
+        pltpu.matmul_push_rhs(small, staging_register=1, mxu_index=n % 2)
+        pltpu.matmul_acc_lhs(sums[n], top, load_staged_rhs=1)
+
+    def halves(value):
+        top = value.astype(jnp.bfloat16)
+        return top, (value - top.astype(jnp.float32)).astype(jnp.bfloat16)
+
+    def prepare(turn, feeding):
+        _, _, j, k = chunk_of((turn + middle_step) % total)
+        load(turn).wait()
+        if feeding:
+            top, rest = halves(xbuf[0, 0, j, k])
         for n in range(tiles):
-            block = stage[step % SLOTS, n * TILE:(n + 1) * TILE, :]
-            top = block.astype(jnp.bfloat16)
-            rest = (block - top.astype(jnp.float32)).astype(jnp.bfloat16)
-            high[index, n] = top.T
-            low[index, n] = rest.T
-
-        @pl.when(step + SLOTS < total)
-        def _():
-            load(step + SLOTS).start()
-
-    def gather(s, h, step, again):
-        _, lane, j, k = chunk_of(step)
+            large, small = halves(stage[turn % SLOTS, n * TILE:(n + 1) * TILE, :])
+            large, small = large.T, small.T
+            high[j * chunks + k, n] = large
+            low[j * chunks + k, n] = small
+            if feeding:
+                feed(n, top, rest, large, small)
+
+        @pl.when(turn + SLOTS < total)
+        def _():
+            load(turn + SLOTS).start()
+
+    def pass_on(s, h, place, again):
+        _, _, j, k = block_of(0, place)
 
         @pl.when(r != c * fanout + j)
         def _():
             copy = relay(s, h, j, k)
             copy.wait_recv()
-
-            @pl.when(lane == x)
+            if again:
+                copy.wait_send()
+            copy.start()
+
+    def gather(s, h, step, again, ahead):
+        if ahead:
+            @pl.when(step + AHEAD < total // 2)
             def _():
-                if again:
-                    copy.wait_send()
-                copy.start()
+                pass_on(s, h, step + AHEAD, again)
+        else:
+            @pl.when(step < total // 2)
+            def _():
+                pass_on(s, h, step, again)
+
+        _, lane, j, k = chunk_of(step)
+
+        @pl.when(lane != x)
+        def _():
+            relay(s, h, j, k).wait_recv()
 
     def multiply(s, h, step):
         _, _, j, k = chunk_of(step)
         index = j * chunks + k
-        value = xbuf[s, h, j, k]
-        top = value.astype(jnp.bfloat16)
-        rest = (value - top.astype(jnp.float32)).astype(jnp.bfloat16)
+        top, rest = halves(xbuf[s, h, j, k])
         for n in range(tiles):
-            pltpu.matmul_push_rhs(high[index, n], staging_register=0, mxu_index=n % 2)
-            pltpu.matmul_acc_lhs(sums[n], top, load_staged_rhs=0)
-            pltpu.matmul_acc_lhs(sums[n], rest)
-            pltpu.matmul_push_rhs(low[index, n], staging_register=1, mxu_index=n % 2)
-            pltpu.matmul_acc_lhs(sums[n], top, load_staged_rhs=1)
+            feed(n, top, rest, high[index, n], low[index, n])
 
     def swap(s, h, k):
         return remote(
@@ -236,6 +273,7 @@
 
             to_makers(s, h, k, lambda copy: copy.start())
 
+    def help_out(s, h):
         @pl.when(aid)
         def _():
             for k in range(chunks):
@@ -279,53 +317,71 @@
 
         swap(last, h, k).wait_send()
 
-    sum_at = SUM_AT * total // 16
-
-    def opening(step, carry):
-        _, _, j, k = chunk_of(step)
-        prepare(step, j * chunks + k)
-        gather(0, 0, step, False)
-        multiply(0, 0, step)
+    sum_at = jnp.where(p == 0, 0, SUM_AT * total // 16)
+    help_at = max(HELP_AT * total // 16, SUM_AT * total // 16)
+
+    def loop(s, h, again, begin, help_on, each, then, start=0):
+        def run_step(step, carry):
+            if begin is not None:
+                @pl.when(step == sum_at)
+                def _():
+                    begin()
+
+            if help_on is not None:
+                @pl.when(step == help_at)
+                def _():
+                    help_on()
+
+            if each is not None:
+                for k in range(chunks):
+                    @pl.when(step == total - chunks + k)
+                    def _(k=k):
+                        each(k)
+
+            gather(s, h, step, again, start == 0)
+            if then is not None:
+                @pl.when(step >= total - AHEAD)
+                def _():
+                    pass_on(*then[:2], step - (total - AHEAD), then[2])
+
+            multiply(s, h, step)
+            return carry
+
+        lax.fori_loop(start, total, run_step, 0)
+        close(s, h)
+
+    def behind(s, h):
+        return functools.partial(add_up, s, h), functools.partial(help_out, s, h), functools.partial(send_out, s, h)
+
+    def following(s, h):
+        return (s, h + 1, True) if h < groups - 1 else (s + 1, 0, True)
+
+    def split(turn, carry):
+        prepare(turn, False)
+        return carry
+
+    def split_and_feed(turn, carry):
+        gather(0, 0, turn + middle_step - total, False, False)
+        prepare(turn, True)
+        return carry
+
+    lax.fori_loop(0, total - middle_step, split, 0)
+    lax.fori_loop(total - middle_step, total, split_and_feed, 0)
+    loop(0, 0, False, None, None, None, (0, 1, False), middle_step)
+    for h in range(1, groups):
+        loop(0, h, False, *behind(0, h - 1), following(0, h))
+
+    def middle(s, carry):
+        loop(s, 0, True, *behind(s - 1, groups - 1), following(s, 0))
         for h in range(1, groups):
-            gather(0, h, step, False)
+            loop(s, h, True, *behind(s, h - 1), following(s, h))
         return carry
 
-    lax.fori_loop(0, total, opening, 0)
-    close(0, 0)
-
-    def loop(s, h, again, begin, each):
-        def run_step(step, carry):
-            if again:
-                gather(s, h, step, True)
-            multiply(s, h, step)
-
-            @pl.when(step == sum_at)
-            def _():
-                begin()
-
-            return carry
-
-        lax.fori_loop(0, total, run_step, 0)
-        close(s, h)
-        for k in range(chunks):
-            each(k)
-
-    def behind(s, h):
-        return functools.partial(add_up, s, h), functools.partial(send_out, s, h)
-
+    lax.fori_loop(1, last, middle, 0)
+    loop(last, 0, True, *behind(last - 1, groups - 1), following(last, 0))
     for h in range(1, groups):
-        loop(0, h, False, *behind(0, h - 1))
-
-    def middle(s, carry):
-        loop(s, 0, True, *behind(s - 1, groups - 1))
-        for h in range(1, groups):
-            loop(s, h, True, *behind(s, h - 1))
-        return carry
-
-    lax.fori_loop(1, last, middle, 0)
-    loop(last, 0, True, *behind(last - 1, groups - 1))
-    for h in range(1, groups):
-        loop(last, h, True, functools.partial(add_up_last, h - 1), functools.partial(finish, h - 1))
+        loop(last, h, True, functools.partial(add_up_last, h - 1), None, functools.partial(finish, h - 1),
+             following(last, h) if h < groups - 1 else None)
     add_up_last(groups - 1)
     for k in range(chunks):
         finish(groups - 1, k)

time: 140 us -> 133 us (0.950)
  Pallas kernels: 138 us -> 131 us
    pallas_call x1, Pallas kernels: 138 us -> 131 us  [local(): pl.pallas_call(functools.partial(kernel, rows, cols, groups), out_shape=j...]
where the time goes in v2:
time: 133 us
  Pallas kernels  131 us (98%)
  local copies, waits for them, and re-layouts  1.67 us (1%)
    pallas_call x1, Pallas kernels, local(): pl.pallas_call(functools.partial(kernel, rows, cols, groups), out_shape=j...  131 us

profile of v2, /device:TPU:0, one launch (start us, length us, event | category | flops | bytes accessed | tf_op | source)
XLA Modules:
  0.0 132.7 jit_solution(1110354664475309322)
XLA Ops:
  0.0 131.0 %shard_map.28 = f32[32,2048]{1,0:T(8,128)} custom-call(f32[2048,8192]{1,0:T(8,128)} %refs_0_.1, f32[32,2048]{1,0:T(8,128)} %refs_1_.1), custom_call_target="tpu_custom_call" | custom-call | tf_op jit(solution)/shard_map/pallas_call | solution.py:427
  131.0 1.7 %copy.4 = f32[32,2048]{1,0:T(8,128)} copy(f32[32,2048]{1,0:T(8,128)} %shard_map.28) | data formatting | bytes 524288

commit v3 on v2

--- a/solution.py
+++ b/solution.py
@@ -14,7 +14,7 @@
 SLOTS = 4
 LAG = 5
 SUM_AT = 3
-HELP_AT = 6
+HELP_AT = 5
 AHEAD = 1
 
 
@@ -273,12 +273,11 @@
 
             to_makers(s, h, k, lambda copy: copy.start())
 
-    def help_out(s, h):
+    def help_out(s, h, k):
         @pl.when(aid)
         def _():
-            for k in range(chunks):
-                sbuf[s + 1, h, k] = column_sum(s, h, k)
-                spread(s + 1, h, k, True)
+            sbuf[s + 1, h, k] = column_sum(s, h, k)
+            spread(s + 1, h, k, True)
 
     def send_out(s, h, k):
         @pl.when(own)
@@ -317,7 +316,7 @@
 
         swap(last, h, k).wait_send()
 
-    sum_at = jnp.where(p == 0, 0, SUM_AT * total // 16)
+    sum_at = jnp.where(p == 0, 1, SUM_AT) * total // 16
     help_at = max(HELP_AT * total // 16, SUM_AT * total // 16)
 
     def loop(s, h, again, begin, help_on, each, then, start=0):
@@ -328,9 +327,10 @@
                     begin()
 
             if help_on is not None:
-                @pl.when(step == help_at)
-                def _():
-                    help_on()
+                for k in range(chunks):
+                    @pl.when(step == min(help_at + k, total - 1))
+                    def _(k=k):
+                        help_on(k)
 
             if each is not None:
                 for k in range(chunks):

time: 133 us -> 130 us (0.977)
  Pallas kernels: 131 us -> 128 us
    pallas_call x1, Pallas kernels: 131 us -> 128 us  [local(): pl.pallas_call(functools.partial(kernel, rows, cols, groups), out_shape=j...]
where the time goes in v3:
time: 130 us; the launch traced here: 129 us
  Pallas kernels  128 us (98%)
  local copies, waits for them, and re-layouts  1.67 us (1%)
    pallas_call x1, Pallas kernels, local(): pl.pallas_call(functools.partial(kernel, rows, cols, groups), out_shape=j...  128 us

profile of v3, /device:TPU:0, one launch (start us, length us, event | category | flops | bytes accessed | tf_op | source)
XLA Modules:
  0.0 129.4 jit_solution(13357268365951029377)
XLA Ops:
  0.0 127.7 %shard_map.28 = f32[32,2048]{1,0:T(8,128)} custom-call(f32[2048,8192]{1,0:T(8,128)} %refs_0_.1, f32[32,2048]{1,0:T(8,128)} %refs_1_.1), custom_call_target="tpu_custom_call" | custom-call | tf_op jit(solution)/shard_map/pallas_call | solution.py:427
  127.7 1.7 %copy.4 = f32[32,2048]{1,0:T(8,128)} copy(f32[32,2048]{1,0:T(8,128)} %shard_map.28) | data formatting | bytes 524288
